TPU v7x, 32 devices: a whole 2x2x4 slice. The times are simulated.
32 devices in a mesh: py: 4 (over y, x), pz: 8 (over z, core).
Axes of the slice: x: 2, y: 2, z: 4, core: 2. Of those that a mesh axis runs over, the one named last changes fastest.
Arguments:
- species: float32 [4, 512, 64, 64], P(None, None, 'py', 'pz'), may hold values from -6 to 6
- coupling: float32 [4, 4], replicated, may hold values from -4 to 4
- symbol_x: float32 [512], replicated, may hold values from 0.3 to 3
- symbol_y: float32 [64], replicated, may hold values from 0.3 to 3
- symbol_z: float32 [64], replicated, may hold values from 0.3 to 3
Outputs:
- modes: float32 [4, 512, 64, 64], P(None, 'py', 'pz')
All inputs are finite; a program needn't handle non-finite values.
Results may differ from a plain program's by a relative error of at most 0.00007.
Values sent between devices are 32-bit elements; how exact they have to be, the bound alone decides.
A program may use at most 64 MiB of HBM per device.

v0:
```python
import jax
import jax.numpy as jnp
from jax import lax
from jax.sharding import PartitionSpec as P


def mode_table(count):
    rank = jnp.arange(count)
    angle = (
        jnp.pi
        / (4 * count)
        * ((2 * rank[:, None] + 1) * (2 * rank[None, :] + 1) % (8 * count)).astype(jnp.float32)
    )
    return jnp.cos(angle) * (2.0 / count) ** 0.5


def transform_dim(values, dim):
    moved = jnp.tensordot(
        values, mode_table(values.shape[dim]), axes=([dim], [0]), precision=lax.Precision.HIGHEST
    )
    return jnp.moveaxis(moved, -1, dim)


def shards(species, coupling, symbol_x, symbol_y, symbol_z):
    part_values = species
    part_values = transform_dim(part_values, 1)
    part_values = lax.all_to_all(part_values, "py", split_axis=1, concat_axis=2, tiled=True)
    part_values = transform_dim(part_values, 2)
    pencil_values = part_values
    pencil_values = lax.all_to_all(pencil_values, "pz", split_axis=2, concat_axis=3, tiled=True)
    pencil_values = transform_dim(pencil_values, 3)
    share_x = pencil_values.shape[1]
    part_x = lax.dynamic_slice_in_dim(symbol_x, lax.axis_index("py") * share_x, share_x)
    share_y = pencil_values.shape[2]
    part_y = lax.dynamic_slice_in_dim(symbol_y, lax.axis_index("pz") * share_y, share_y)
    symbol = part_x[:, None, None] + part_y[None, :, None] + symbol_z[None, None, :]
    weight_xyz = 1.0 / (1.0 + symbol)
    mixed_fields = jnp.einsum(
        "ab,bxyz->axyz", coupling, pencil_values, precision=lax.Precision.HIGHEST
    )
    pencil_values = weight_xyz * pencil_values + (1.0 - weight_xyz) * mixed_fields
    return pencil_values


def solution(mesh):
    return jax.shard_map(
        shards,
        mesh=mesh,
        in_specs=(P(None, None, "py", "pz"), P(), P(), P(), P()),
        out_specs=P(None, "py", "pz", None),
        check_vma=False,
    )
```

profile of v0, /device:TPU:0, one launch (start us, length us, event | category | flops | bytes accessed | tf_op | source)
XLA Modules:
  0.0 95.0 jit_solution(6037659753878143256)
XLA Ops:
  0.0 0.0 copy-start
  0.0 1.2 %copy-done = f32[4,512,16,8]{1,3,2,0:T(8,128)S(1)} copy-done((f32[4,512,16,8]{1,3,2,0:T(8,128)S(1)}, f32[4,512,16,8]{1,3,2,0:T(8,128)}, u32[]{:S(2)}) %copy-start) | copy-done | bytes 1048600
  1.2 6.2 %convolution_bitcast_fusion.1 = f32[4,512,16,8]{1,2,3,0:T(8,128)S(1)} fusion(f32[4,512,16,8]{1,3,2,0:T(8,128)S(1)} %copy-done, s32[512]{0:T(512)S(1)} %multiply_add_fusion), kind=kOutput, calls=%fused_computation.6 | convolution fusion | flops 1614544896 | bytes 2099200 | tf_op jit(solution)/shard_map/dot_general | solution.py:18
  7.4 7.5 %copy.12 = f32[4,512,16,8]{2,3,0,1:T(8,128)} copy(f32[4,512,16,8]{1,2,3,0:T(8,128)S(1)} %convolution_bitcast_fusion.1) | data formatting | bytes 2097152 | tf_op jit(solution)/shard_map/transpose | solution.py:21
  14.9 6.4 %reshape.68 = f32[4,1,65536]{2,1,0:T(1,128)} reshape(f32[512,4,8,16]{3,2,1,0:T(8,128)} %bitcast.35) | data formatting | bytes 2097152
  21.3 5.2 %all-to-all-start = ((f32[4,1,65536]{2,1,0:T(1,128)}), f32[4,1,65536]{2,1,0:T(1,128)S(1)}, u32[]{:S(2)}, u32[]{:S(2)}) async-start(f32[4,1,65536]{2,1,0:T(1,128)} %reshape.68), calls=%async_computation | async-start | bytes 2097152 | tf_op jit(solution)/shard_map/all_to_all | solution.py:27
  26.5 13.6 %all-to-all-done = f32[4,1,65536]{2,1,0:T(1,128)S(1)} async-done(((f32[4,1,65536]{2,1,0:T(1,128)}), f32[4,1,65536]{2,1,0:T(1,128)S(1)}, u32[]{:S(2)}, u32[]{:S(2)}) %all-to-all-start) | async-done | bytes 1048608 | tf_op jit(solution)/shard_map/all_to_all | solution.py:27
  40.1 0.5 broadcast.168
  40.6 3.7 %reduce = f32[4,65536]{1,0:T(4,128)S(1)} reduce(f32[4,1,65536]{2,1,0:T(1,128)S(1)} %all-to-all-done, f32[]{:T(128)} %broadcast.168), dimensions={1}, to_apply=%all_to_all.26.reduce_sub_computation | reduce | bytes 2097156 | tf_op jit(solution)/shard_map/all_to_all | solution.py:27
  44.3 6.1 %reshape.69 = f32[512,4,8,16]{3,2,1,0:T(8,128)} reshape(f32[4,65536]{1,0:T(4,128)S(1)} %reduce) | data formatting | bytes 2097152
  50.5 0.0 copy-start.3
  50.5 0.0 copy-start.2
  50.5 0.0 copy-start.1
  50.5 5.2 %copy.13 = f32[4,4,128,16,8]{2,3,1,4,0:T(8,128)S(1)} copy(f32[4,4,128,16,8]{3,4,0,2,1:T(8,128)} %bitcast.36) | data formatting | bytes 2097152 | tf_op jit(solution)/shard_map/all_to_all | solution.py:27
  55.6 1.3 %convolution_bitcast_fusion = f32[4,128,64,8]{1,2,3,0:T(8,128)S(1)} fusion(f32[4,128,64,8]{1,2,3,0:T(8,128)S(1)} %bitcast.37, s32[64]{0:T(128)S(1)} %multiply_add_fusion.1), kind=kOutput, calls=%fused_computation.5 | convolution fusion | flops 201388032 | bytes 2097408 | tf_op jit(solution)/shard_map/dot_general | solution.py:18
  56.9 1.6 %copy.14 = f32[4,128,64,8]{1,3,0,2:T(8,128)} copy(f32[4,128,64,8]{1,2,3,0:T(8,128)S(1)} %convolution_bitcast_fusion) | data formatting | bytes 2097152 | tf_op jit(solution)/shard_map/transpose | solution.py:21
  58.5 4.9 %all-to-all-start.1 = ((f32[4,128,64,8]{1,3,0,2:T(8,128)}), f32[4,128,64,8]{1,3,0,2:T(8,128)S(1)}, u32[]{:S(2)}, u32[]{:S(2)}) async-start(f32[4,128,64,8]{1,3,0,2:T(8,128)} %copy.14), calls=%async_computation.1 | async-start | bytes 2097152 | tf_op jit(solution)/shard_map/all_to_all | solution.py:30
  63.4 0.0 copy-done.3
  63.4 0.1 dynamic_slice.7
  63.5 0.8 dynamic_slice.6
  64.3 0.1 broadcast_add_fusion
  64.4 0.0 copy-done.2
  64.4 0.1 add_divide_fusion
  64.5 25.5 %all-to-all-done.1 = f32[4,128,64,8]{1,3,0,2:T(8,128)S(1)} async-done(((f32[4,128,64,8]{1,3,0,2:T(8,128)}), f32[4,128,64,8]{1,3,0,2:T(8,128)S(1)}, u32[]{:S(2)}, u32[]{:S(2)}) %all-to-all-start.1) | async-done | bytes 1048608 | tf_op jit(solution)/shard_map/all_to_all | solution.py:30
  90.0 1.3 %fusion.7 = f32[4,128,8,64]{1,3,2,0:T(8,128)S(1)} fusion(f32[4,128,8,8,8]{1,4,0,3,2:T(8,128)S(1)} %bitcast.38, s32[64]{0:T(128)S(1)} %multiply_add_fusion.1), kind=kOutput, calls=%fused_computation.13 | convolution fusion | flops 201388032 | bytes 2097408 | tf_op jit(solution)/shard_map/dot_general | solution.py:18
  91.3 0.0 copy-done.1
  91.3 2.5 %fusion.9 = f32[128,8,64,4]{0,3,2,1:T(4,128)S(1)} fusion(f32[4,128,8,64]{1,3,2,0:T(8,128)S(1)} %fusion.7, f32[4,4]{1,0:T(4,128)S(1)} %copy-done.1), kind=kOutput, calls=%fused_computation.17 | convolution fusion | flops 12582912 | bytes 2097216 | tf_op jit(solution)/shard_map/ab,bxyz->axyz/dot_general | solution.py:38
  93.8 1.2 %bitcast_add_fusion = f32[4,128,8,64]{1,3,2,0:T(8,128)} fusion(f32[128,8,64,4]{0,3,2,1:T(4,128)S(1)} %fusion.9, f32[4,128,8,64]{1,3,2,0:T(8,128)S(1)} %fusion.7, f32[128,8,64]{0,2,1:T(8,128)S(1)} %get-tuple-element.6, f32[128,8,64]{0,2,1:T(8,128)S(1)} %get-tuple-element.5), kind=kLoop, calls=%fused_computation.15 | loop fusion | flops 786432 | bytes 3670016 | tf_op jit(solution)/shard_map/add | solution.py:41
  (2 shorter events, 0.0 us)
Async XLA Ops:
  0.0 1.2 %copy-start = (f32[4,512,16,8]{1,3,2,0:T(8,128)S(1)}, f32[4,512,16,8]{1,3,2,0:T(8,128)}, u32[]{:S(2)}) copy-start(f32[4,512,16,8]{1,3,2,0:T(8,128)} %param.5) | copy-start | bytes 3145732
  21.3 18.8 %all-to-all-start = ((f32[4,1,65536]{2,1,0:T(1,128)}), f32[4,1,65536]{2,1,0:T(1,128)S(1)}, u32[]{:S(2)}, u32[]{:S(2)}) async-start(f32[4,1,65536]{2,1,0:T(1,128)} %reshape.68), calls=%async_computation | async-start | bytes 2097152 | tf_op jit(solution)/shard_map/all_to_all | solution.py:27
  50.5 13.0 %copy-start.3 = (f32[64]{0:T(128)S(1)}, f32[64]{0:T(128)}, u32[]{:S(2)}) copy-start(f32[64]{0:T(128)} %param.8) | copy-start | bytes 772
  50.5 13.9 %copy-start.2 = (f32[64]{0:T(128)S(1)}, f32[64]{0:T(128)}, u32[]{:S(2)}) copy-start(f32[64]{0:T(128)} %param.9) | copy-start | bytes 772
  50.5 40.8 %copy-start.1 = (f32[4,4]{1,0:T(4,128)S(1)}, f32[4,4]{1,0:T(4,128)}, u32[]{:S(2)}) copy-start(f32[4,4]{1,0:T(4,128)} %param.6) | copy-start | bytes 196
  58.5 31.5 %all-to-all-start.1 = ((f32[4,128,64,8]{1,3,0,2:T(8,128)}), f32[4,128,64,8]{1,3,0,2:T(8,128)S(1)}, u32[]{:S(2)}, u32[]{:S(2)}) async-start(f32[4,128,64,8]{1,3,0,2:T(8,128)} %copy.14), calls=%async_computation.1 | async-start | bytes 2097152 | tf_op jit(solution)/shard_map/all_to_all | solution.py:30
where the time goes:
time: 95.4 us; the launch traced here: 95 us
  waiting for transfers between devices  39.1 us (41%)
  local copies, waits for them, and re-layouts  29.3 us (31%)
  matrix products  11.2 us (12%)
  starting transfers between devices  10.1 us (11%)
  other arithmetic  5.07 us (5%)
    all_to_all x1, waiting for transfers between devices, shards(): lax.all_to_all(pencil_values, 'pz', split_axis=2, concat_axis=3, tiled=True)  25.5 us
    unnamed x10, local copies, waits for them, and re-layouts  13.8 us
    all_to_all x1, waiting for transfers between devices, shards(): lax.all_to_all(part_values, 'py', split_axis=1, concat_axis=2, tiled=True)  13.6 us
    transpose x2, local copies, waits for them, and re-layouts, transform_dim(): return jnp.moveaxis(moved, -1, dim)  9.07 us
    dot_general x3, matrix products, transform_dim(): jnp.tensordot(values, mode_table(values.shape[dim]), axes=([dim], [0]), p...  8.73 us
    all_to_all x2, local copies, waits for them, and re-layouts, shards(): lax.all_to_all(part_values, 'py', split_axis=1, concat_axis=2, tiled=True)  5.68 us
    all_to_all x1, starting transfers between devices, shards(): lax.all_to_all(part_values, 'py', split_axis=1, concat_axis=2, tiled=True)  5.19 us
    all_to_all x1, starting transfers between devices, shards(): lax.all_to_all(pencil_values, 'pz', split_axis=2, concat_axis=3, tiled=True)  4.93 us
  transfers between devices with their start and end apart: 2, of which 2 were waited for; matrix products, arithmetic and copies ran while one was open for 1% of the time, Pallas kernels for 0%

commit v1 on v0

--- a/solution.py
+++ b/solution.py
@@ -24,7 +24,10 @@
 def shards(species, coupling, symbol_x, symbol_y, symbol_z):
     part_values = species
     part_values = transform_dim(part_values, 1)
-    part_values = lax.all_to_all(part_values, "py", split_axis=1, concat_axis=2, tiled=True)
+    part_values = jnp.concatenate(
+        lax.all_to_all(jnp.stack(jnp.split(part_values, lax.axis_size("py"), axis=1)), "py", 0, 0),
+        axis=2,
+    )
     part_values = transform_dim(part_values, 2)
     pencil_values = part_values
     pencil_values = lax.all_to_all(pencil_values, "pz", split_axis=2, concat_axis=3, tiled=True)

time: 95.4 us -> 67.5 us (0.71)
  local copies, waits for them, and re-layouts: 29.3 us -> 5.31 us
  other arithmetic: 5.07 us -> 2.45 us
  waiting for transfers between devices: 39.1 us -> 37.9 us
    unnamed x10 -> x8, local copies, waits for them, and re-layouts: 13.8 us -> 2.46 us
    transpose x2 -> x1, local copies, waits for them, and re-layouts: 9.07 us -> 1.58 us  [transform_dim(): return jnp.moveaxis(moved, -1, dim)]
    all_to_all x2 -> x0, local copies, waits for them, and re-layouts: 5.68 us -> none  [shards(): lax.all_to_all(part_values, 'py', split_axis=1, concat_axis=2, tiled=True)]
    all_to_all x1 -> x0, other arithmetic: 3.68 us -> none  [shards(): lax.all_to_all(part_values, 'py', split_axis=1, concat_axis=2, tiled=True)]
    all_to_all x1, waiting for transfers between devices: 25.5 us -> 24.3 us  [shards(): lax.all_to_all(pencil_values, 'pz', split_axis=2, concat_axis=3, tiled=True)]
    another operation x0 -> x1, other arithmetic: none -> 1.07 us  [shards(): jnp.stack(jnp.split(part_values, lax.axis_size('py'), axis=1))]
  transfers between devices with their start and end apart: 2 -> 2, of which waited for: 2 -> 2; matrix products, arithmetic and copies ran while one was open for 1% -> 2% of each run, Pallas kernels for 0% -> 0%
where the time goes in v1:
time: 67.5 us; the launch traced here: 67.2 us
  waiting for transfers between devices  37.9 us (56%)
  matrix products  11.3 us (17%)
  starting transfers between devices  10.1 us (15%)
  local copies, waits for them, and re-layouts  5.31 us (8%)
  other arithmetic  2.45 us (4%)
    all_to_all x1, waiting for transfers between devices, shards(): lax.all_to_all(pencil_values, 'pz', split_axis=2, concat_axis=3, tiled=True)  24.3 us
    all_to_all x1, waiting for transfers between devices, shards(): lax.all_to_all(jnp.stack(jnp.split(part_values, lax.axis_size('py'), axis...  13.6 us
    dot_general x3, matrix products, transform_dim(): jnp.tensordot(values, mode_table(values.shape[dim]), axes=([dim], [0]), p...  8.81 us
    all_to_all x1, starting transfers between devices, shards(): lax.all_to_all(jnp.stack(jnp.split(part_values, lax.axis_size('py'), axis...  5.19 us
    all_to_all x1, starting transfers between devices, shards(): lax.all_to_all(pencil_values, 'pz', split_axis=2, concat_axis=3, tiled=True)  4.93 us
    dot_general x1, matrix products, shards(): jnp.einsum('ab,bxyz->axyz', coupling, pencil_values, precision=lax.Precis...  2.48 us
    unnamed x8, local copies, waits for them, and re-layouts  2.46 us
    transpose x1, local copies, waits for them, and re-layouts, transform_dim(): return jnp.moveaxis(moved, -1, dim)  1.58 us
  transfers between devices with their start and end apart: 2, of which 2 were waited for; matrix products, arithmetic and copies ran while one was open for 2% of the time, Pallas kernels for 0%

profile of v1, /device:TPU:0, one launch (start us, length us, event | category | flops | bytes accessed | tf_op | source)
XLA Modules:
  0.0 67.2 jit_solution(9824811709457195339)
XLA Ops:
  0.0 0.0 copy-start
  0.0 1.2 %copy-done = f32[4,512,16,8]{1,3,2,0:T(8,128)S(1)} copy-done((f32[4,512,16,8]{1,3,2,0:T(8,128)S(1)}, f32[4,512,16,8]{1,3,2,0:T(8,128)}, u32[]{:S(2)}) %copy-start) | copy-done | bytes 1048600
  1.2 6.2 %convolution_bitcast_fusion.1 = f32[4,512,16,8]{1,2,3,0:T(8,128)S(1)} fusion(f32[4,512,16,8]{1,3,2,0:T(8,128)S(1)} %copy-done, s32[512]{0:T(512)S(1)} %multiply_add_fusion), kind=kOutput, calls=%fused_computation.6 | convolution fusion | flops 1614544896 | bytes 2099200 | tf_op jit(solution)/shard_map/dot_general | solution.py:18
  7.4 0.1 slice_bitcast_fusion.3
  7.5 1.1 %pad_maximum_fusion = f32[4,4,128,16,8]{2,3,4,1,0:T(8,128)} fusion(f32[1,4,128,16,8]{2,3,4,1,0:T(8,128)S(1)} %get-tuple-element.6, f32[1,4,128,16,8]{2,3,4,1,0:T(8,128)S(1)} %get-tuple-element.7, f32[1,4,128,16,8]{2,3,4,1,0:T(8,128)S(1)} %get-tuple-element.8, f32[1,4,128,16,8]{2,3,4,1,0:T(8,128)S(1)} %get-tuple-element.5), kind=kLoop, calls=%fused_computation.13 | loop fusion | flops 786432 | bytes 2097152 | tf_op jit(solution)/shard_map/stack | solution.py:28
  8.6 5.2 %all-to-all-start = ((f32[4,4,128,16,8]{2,3,4,1,0:T(8,128)}), f32[4,4,128,16,8]{2,3,4,1,0:T(8,128)S(1)}, u32[]{:S(2)}, u32[]{:S(2)}) async-start(f32[4,4,128,16,8]{2,3,4,1,0:T(8,128)} %pad_maximum_fusion), calls=%async_computation | async-start | bytes 2097152 | tf_op jit(solution)/shard_map/all_to_all | solution.py:28
  13.8 13.6 %all-to-all-done = f32[4,4,128,16,8]{2,3,4,1,0:T(8,128)S(1)} async-done(((f32[4,4,128,16,8]{2,3,4,1,0:T(8,128)}), f32[4,4,128,16,8]{2,3,4,1,0:T(8,128)S(1)}, u32[]{:S(2)}, u32[]{:S(2)}) %all-to-all-start) | async-done | bytes 1048608 | tf_op jit(solution)/shard_map/all_to_all | solution.py:28
  27.4 0.3 copy.17
  27.7 1.4 %convolution_bitcast_fusion = f32[4,128,64,8]{1,2,3,0:T(8,128)S(1)} fusion(f32[4,128,64,8]{1,3,2,0:T(8,128)S(1)} %bitcast.40, s32[64]{0:T(128)S(1)} %multiply_add_fusion.1), kind=kOutput, calls=%fused_computation.5 | convolution fusion | flops 201388032 | bytes 2097408 | tf_op jit(solution)/shard_map/dot_general | solution.py:18
  29.1 1.6 %copy.19 = f32[4,128,64,8]{1,3,0,2:T(8,128)} copy(f32[4,128,64,8]{1,2,3,0:T(8,128)S(1)} %convolution_bitcast_fusion) | data formatting | bytes 2097152 | tf_op jit(solution)/shard_map/transpose | solution.py:21
  30.7 4.9 %all-to-all-start.1 = ((f32[4,128,64,8]{1,3,0,2:T(8,128)}), f32[4,128,64,8]{1,3,0,2:T(8,128)S(1)}, u32[]{:S(2)}, u32[]{:S(2)}) async-start(f32[4,128,64,8]{1,3,0,2:T(8,128)} %copy.19), calls=%async_computation.1 | async-start | bytes 2097152 | tf_op jit(solution)/shard_map/all_to_all | solution.py:33
  35.6 0.0 copy-start.3
  35.6 0.6 copy-done.3
  36.3 0.1 dynamic_slice.7
  36.4 0.8 %dynamic_slice.6 = f32[128]{0:T(128)S(1)} dynamic-slice(f32[512]{0:T(512)} %param.7, s32[]{:T(128)S(6)} %select_n.23), dynamic_slice_sizes={128} | dynamic-slice | bytes 1028 | tf_op jit(solution)/shard_map/dynamic_slice | solution.py:36
  37.1 0.0 copy-start.2
  37.1 0.1 broadcast_add_fusion
  37.2 0.6 copy-done.2
  37.8 0.1 add_divide_fusion
  37.9 24.3 %all-to-all-done.1 = f32[4,128,64,8]{1,3,0,2:T(8,128)S(1)} async-done(((f32[4,128,64,8]{1,3,0,2:T(8,128)}), f32[4,128,64,8]{1,3,0,2:T(8,128)S(1)}, u32[]{:S(2)}, u32[]{:S(2)}) %all-to-all-start.1) | async-done | bytes 1048608 | tf_op jit(solution)/shard_map/all_to_all | solution.py:33
  62.2 0.0 copy-start.1
  62.2 1.3 %fusion.7 = f32[4,128,8,64]{1,3,2,0:T(8,128)S(1)} fusion(f32[4,128,8,8,8]{1,4,0,3,2:T(8,128)S(1)} %bitcast.39, s32[64]{0:T(128)S(1)} %multiply_add_fusion.1), kind=kOutput, calls=%fused_computation.14 | convolution fusion | flops 201388032 | bytes 2097408 | tf_op jit(solution)/shard_map/dot_general | solution.py:18
  63.5 0.0 copy-done.1
  63.5 2.5 %fusion.9 = f32[128,8,64,4]{0,3,2,1:T(4,128)S(1)} fusion(f32[4,128,8,64]{1,3,2,0:T(8,128)S(1)} %fusion.7, f32[4,4]{1,0:T(4,128)S(1)} %copy-done.1), kind=kOutput, calls=%fused_computation.18 | convolution fusion | flops 12582912 | bytes 2097216 | tf_op jit(solution)/shard_map/ab,bxyz->axyz/dot_general | solution.py:41
  66.0 1.2 %bitcast_add_fusion = f32[4,128,8,64]{1,3,2,0:T(8,128)} fusion(f32[128,8,64,4]{0,3,2,1:T(4,128)S(1)} %fusion.9, f32[4,128,8,64]{1,3,2,0:T(8,128)S(1)} %fusion.7, f32[128,8,64]{0,2,1:T(8,128)S(1)} %get-tuple-element.10, f32[128,8,64]{0,2,1:T(8,128)S(1)} %get-tuple-element.9), kind=kLoop, calls=%fused_computation.16 | loop fusion | flops 786432 | bytes 3670016 | tf_op jit(solution)/shard_map/add | solution.py:44
  (2 shorter events, 0.0 us)
Async XLA Ops:
  0.0 1.2 %copy-start = (f32[4,512,16,8]{1,3,2,0:T(8,128)S(1)}, f32[4,512,16,8]{1,3,2,0:T(8,128)}, u32[]{:S(2)}) copy-start(f32[4,512,16,8]{1,3,2,0:T(8,128)} %param.5) | copy-start | bytes 3145732
  8.6 18.8 %all-to-all-start = ((f32[4,4,128,16,8]{2,3,4,1,0:T(8,128)}), f32[4,4,128,16,8]{2,3,4,1,0:T(8,128)S(1)}, u32[]{:S(2)}, u32[]{:S(2)}) async-start(f32[4,4,128,16,8]{2,3,4,1,0:T(8,128)} %pad_maximum_fusion), calls=%async_computation | async-start | bytes 2097152 | tf_op jit(solution)/shard_map/all_to_all | solution.py:28
  30.7 31.5 %all-to-all-start.1 = ((f32[4,128,64,8]{1,3,0,2:T(8,128)}), f32[4,128,64,8]{1,3,0,2:T(8,128)S(1)}, u32[]{:S(2)}, u32[]{:S(2)}) async-start(f32[4,128,64,8]{1,3,0,2:T(8,128)} %copy.19), calls=%async_computation.1 | async-start | bytes 2097152 | tf_op jit(solution)/shard_map/all_to_all | solution.py:33
  35.6 0.7 copy-start.3
  37.1 0.7 copy-start.2
  62.2 1.3 %copy-start.1 = (f32[4,4]{1,0:T(4,128)S(1)}, f32[4,4]{1,0:T(4,128)}, u32[]{:S(2)}) copy-start(f32[4,4]{1,0:T(4,128)} %param.6) | copy-start | bytes 196
